TPU v7x, 32 devices: a 4x4x1 block of a 4x4x8 slice. The times are simulated.
32 devices in a mesh: dp: 1 (over z), ep: 32 (over y, x, core).
Axes of the slice: x: 4, y: 4, z: 1, core: 2. Of those that a mesh axis runs over, the one named last changes fastest.
The devices are a block of a 4x4x8 slice.
Arguments:
- x_in: bfloat16 [32768, 2048], P(('dp', 'ep'))
- norm_gain: bfloat16 [2048], replicated
- w_router: bfloat16 [2048, 64], replicated
- expert_ids: int32 [32768, 6], P(('dp', 'ep'))
- w_gate: bfloat16 [64, 2048, 1408], P('ep')
- w_up: bfloat16 [64, 2048, 1408], P('ep')
- w_down: bfloat16 [64, 1408, 2048], P('ep')
Outputs:
- output: bfloat16 [32768, 2048], P(('dp', 'ep'))
All inputs are finite; a program needn't handle non-finite values.
Results may differ from a plain program's by a relative error of at most 0.0012.
Values are sent between devices in bfloat16 or wider.
A program may use at most 768 MiB of HBM per device.

v0:
```python
import jax
import jax.numpy as jnp
from jax import lax
from jax.sharding import PartitionSpec as P

EPS = 1e-6


def norm_and_gates(x_in, norm_gain, w_router, expert_ids):
    resid = x_in.astype(jnp.float32)
    mean_sq = jnp.mean(resid * resid, axis=-1, keepdims=True)
    normed = (resid * lax.rsqrt(mean_sq + EPS) * norm_gain.astype(jnp.float32)).astype(jnp.bfloat16)
    logits = jnp.dot(normed, w_router, preferred_element_type=jnp.float32)
    router_p = jax.nn.softmax(logits, axis=-1)
    picked = jnp.take_along_axis(router_p, expert_ids, axis=1)
    gates = picked / jnp.sum(picked, axis=1, keepdims=True)
    return resid, normed, gates


def route_slots(expert_ids, experts, capacity):
    flat_ids = expert_ids.reshape(-1)
    onehot = (flat_ids[:, None] == jnp.arange(experts, dtype=jnp.int32)[None, :]).astype(jnp.int32)
    before = jnp.cumsum(onehot, axis=0) - onehot
    position = jnp.sum(before * onehot, axis=1)
    return flat_ids * capacity + position


def expert_mlp(rows, w_gate, w_up, w_down):
    gate_val = jnp.einsum("erd,edf->erf", rows, w_gate, preferred_element_type=jnp.float32)
    up_val = jnp.einsum("erd,edf->erf", rows, w_up, preferred_element_type=jnp.float32)
    hidden_act = (jax.nn.silu(gate_val) * up_val).astype(jnp.bfloat16)
    return jnp.einsum("erf,efd->erd", hidden_act, w_down, preferred_element_type=jnp.float32).astype(jnp.bfloat16)


def solution(mesh):
    def local_block(x_in, norm_gain, w_router, expert_ids, w_gate, w_up, w_down):
        tokens, hidden = x_in.shape
        experts = w_router.shape[1]
        top_k = expert_ids.shape[1]
        capacity = 2 * tokens * top_k // experts
        resid, normed, gates = norm_and_gates(x_in, norm_gain, w_router, expert_ids)
        slots = route_slots(expert_ids, experts, capacity)
        choice_tok = jnp.arange(tokens * top_k, dtype=jnp.int32) // top_k
        slot_tok = jnp.full((experts * capacity,), tokens, jnp.int32).at[slots].set(choice_tok)
        outgoing = jnp.take(normed, slot_tok, axis=0, mode="fill", fill_value=0).reshape(experts, capacity, hidden)
        received = lax.all_to_all(outgoing, "ep", 0, 1, tiled=True)
        outputs = expert_mlp(received, w_gate, w_up, w_down)
        returned = lax.all_to_all(outputs, "ep", 1, 0, tiled=True).reshape(experts * capacity, hidden)
        y_sel = jnp.take(returned, slots, axis=0).reshape(tokens, top_k, hidden)
        mixed = jnp.sum(y_sel.astype(jnp.float32) * gates[:, :, None], axis=1)
        return (resid + mixed).astype(jnp.bfloat16)

    tok_spec = P(("dp", "ep"), None)
    expert_spec = P("ep", None, None)
    return jax.shard_map(local_block, mesh=mesh, in_specs=(tok_spec, P(None), P(None, None), tok_spec, expert_spec, expert_spec, expert_spec), out_specs=tok_spec, check_vma=False)
```

profile of v0, /device:TPU:96, one launch (start us, length us, event | category | flops | bytes accessed | tf_op | source)
XLA Modules:
  0.0 2044.4 jit_solution(8008031136938973353)
XLA Ops:
  0.8 1.0 copy.36
  3.2 18.8 reduce-window.6
  23.9 0.8 fusion.6
  25.9 23.0 %scatter_custom_fusion = s32[12288]{0:T(1024)S(1)} fusion(s32[6144]{0:T(1024)S(1)} %bitcast.52, s32[6144]{0:T(1024)S(1)} %add_select_fusion, s32[]{:T(128)} %constant.47.clone.1), kind=kCustom, calls=%fused_computation.41 | custom fusion | bytes 49156 | tf_op jit(solution)/shard_map/scatter | solution.py:44
  49.0 3.1 fusion
  52.2 5.2 fusion.2
  57.4 94.1 %gather_fusion = bf16[12288,2048]{1,0:T(8,128)(2,1)} fusion(bf16[1024,2048]{1,0:T(8,128)(2,1)} %fusion.2, s32[12288]{0:T(1024)S(1)} %fusion.10), kind=kCustom, calls=%fused_computation | custom fusion | bytes 100712448 | tf_op jit(solution)/shard_map/jit(_take)/gather | solution.py:45
  151.5 33.8 %broadcast_select_fusion = bf16[64,192,2048]{2,1,0:T(8,128)(2,1)} fusion(bf16[64,192,2048]{2,1,0:T(8,128)(2,1)} %bitcast.45, pred[64,192]{1,0:T(8,128)(4,1)S(1)} %broadcast_in_dim.41), kind=kLoop, calls=%fused_computation.6 | loop fusion | flops 25165824 | bytes 100675584 | tf_op jit(solution)/shard_map/jit(_take)/select_n | solution.py:45
  185.2 553.2 %all_to_all.33 = bf16[64,192,2048]{2,1,0:T(8,128)(2,1)} all-to-all(bf16[64,192,2048]{2,1,0:T(8,128)(2,1)} %broadcast_select_fusion), channel_id=1, replica_groups=mesh['dp'=1,'ep'=32] {'ep'}, dimensions={0} | all-to-all | bytes 100663296 | tf_op jit(solution)/shard_map/all_to_all | solution.py:46
  738.5 33.4 %copy.43 = bf16[2,32,192,2048]{3,2,1,0:T(8,128)(2,1)} copy(bf16[2,32,192,2048]{3,2,0,1:T(8,128)(2,1)} %bitcast.44) | data formatting | bytes 100663296 | tf_op jit(solution)/shard_map/all_to_all | solution.py:46
  771.8 87.8 %fusion.18 = f32[2,6144,1408]{2,1,0:T(8,128)} fusion(bf16[2,6144,2048]{2,1,0:T(8,128)(2,1)} %bitcast.46, bf16[2,2048,1408]{2,1,0:T(8,128)(2,1)} %param.11), kind=kOutput, calls=%fused_computation.50 | convolution fusion | flops 70866960384 | bytes 131072000 | tf_op jit(solution)/shard_map/erd,edf->erf/dot_general | solution.py:29
  859.6 91.6 %multiply_convert_fusion = bf16[2,6144,1408]{2,1,0:T(8,128)(2,1)} fusion(f32[2,6144,1408]{2,1,0:T(8,128)} %fusion.18, bf16[2,6144,2048]{2,1,0:T(8,128)(2,1)} %bitcast.47, bf16[2,2048,1408]{2,1,0:T(8,128)(2,1)} %param.12), kind=kOutput, calls=%fused_computation.4 | convolution fusion | flops 70970769408 | bytes 165675008 | tf_op jit(solution)/shard_map/erd,edf->erf/dot_general | solution.py:30
  951.2 87.3 %convolution_convert_fusion = bf16[2,6144,2048]{2,1,0:T(8,128)(2,1)} fusion(bf16[2,6144,1408]{2,1,0:T(8,128)(2,1)} %multiply_convert_fusion, bf16[2,1408,2048]{2,1,0:T(8,128)(2,1)} %param.13), kind=kOutput, calls=%fused_computation.7 | convolution fusion | flops 70892126208 | bytes 96468992 | tf_op jit(solution)/shard_map/erf,efd->erd/dot_general | solution.py:32
  1038.4 89.5 %copy.44 = bf16[2,6144,2048]{2,0,1:T(2,128)(2,1)} copy(bf16[2,6144,2048]{2,1,0:T(8,128)(2,1)} %convolution_convert_fusion) | data formatting | bytes 100663296 | tf_op jit(solution)/shard_map/convert_element_type | solution.py:32
  1127.9 5.6 all-to-all-start.1
  1133.6 1.3 reduce_sum.50
  1135.5 3.6 fusion.17
  1139.2 49.3 %gather_fusion.2 = f32[6144]{0:T(1024)S(1)} fusion(f32[1024,64]{0,1:T(8,128)S(1)} %fusion.8, s32[6144]{0:T(1024)S(1)} %reshape.129), kind=kCustom, calls=%fused_computation.2 | custom fusion | bytes 98304 | tf_op jit(solution)/shard_map/jit(take_along_axis)/gather | solution.py:15
  1190.0 589.9 %all-to-all-done.1 = bf16[2,6144,2048]{2,0,1:T(2,128)(2,1)} async-done(((bf16[2,6144,2048]{2,0,1:T(2,128)(2,1)}), bf16[2,6144,2048]{2,0,1:T(2,128)(2,1)}, u32[]{:S(2)}, u32[]{:S(2)}) %all-to-all-start.1) | async-done | bytes 50331680 | tf_op jit(solution)/shard_map/all_to_all | solution.py:48
  1779.9 33.6 %copy.45 = bf16[2,32,192,2048]{3,2,0,1:T(8,128)(2,1)} copy(bf16[2,32,192,2048]{3,0,2,1:T(2,128)(2,1)} %bitcast.9) | data formatting | bytes 100663296 | tf_op jit(solution)/shard_map/all_to_all | solution.py:48
  1813.5 143.1 %gather_fusion.1 = bf16[6144,2048]{1,0:T(8,128)(2,1)} fusion(bf16[12288,2048]{1,0:T(8,128)(2,1)} %bitcast.43, s32[6144]{0:T(1024)S(1)} %broadcast_clamp_fusion), kind=kCustom, calls=%fused_computation.1 | custom fusion | bytes 50356224 | tf_op jit(solution)/shard_map/jit(_take)/gather | solution.py:49
  1956.7 39.4 %gather.19 = bf16[1024,6,2048]{2,1,0:T(8,128)(2,1)} reshape(bf16[6144,2048]{1,0:T(8,128)(2,1)} %gather_fusion.1) | data formatting | bytes 50331648 | tf_op jit(solution)/shard_map/jit(_take)/gather | solution.py:49
  1996.1 39.7 %multiply_reduce_fusion = f32[1024,2048]{1,0:T(8,128)} fusion(f32[1024,6]{1,0:T(8,128)S(1)} %copy.48, bf16[1024,6,2048]{2,1,0:T(8,128)(2,1)} %gather.19, pred[1024,6]{1,0:T(8,128)(4,1)S(1)} %copy.41), kind=kLoop, calls=%fused_computation.5 | loop fusion | flops 48234496 | bytes 33585152 | tf_op jit(solution)/shard_map/reduce_sum | solution.py:50
  2035.8 8.3 fusion.3
  (49 shorter events, 7.5 us)
Async XLA Ops:
  0.0 1135.4 %copy-start = (bf16[2048,64]{0,1:T(8,128)(2,1)S(1)}, bf16[2048,64]{0,1:T(8,128)(2,1)}, u32[]{:S(2)}) copy-start(bf16[2048,64]{0,1:T(8,128)(2,1)} %param.9) | copy-start | bytes 786436
  0.0 49.0 %copy-start.8 = (bf16[2048]{0:T(1024)(128)(2,1)S(1)}, bf16[2048]{0:T(1024)(128)(2,1)}, u32[]{:S(2)}) copy-start(bf16[2048]{0:T(1024)(128)(2,1)} %param.8) | copy-start | bytes 12292
  24.7 0.6 copy-start.4
  25.3 0.6 copy-start.6
  1127.9 5.7 copy-start.5
  1127.9 6.9 copy-start.2
  1127.9 652.0 %all-to-all-start.1 = ((bf16[2,6144,2048]{2,0,1:T(2,128)(2,1)}), bf16[2,6144,2048]{2,0,1:T(2,128)(2,1)}, u32[]{:S(2)}, u32[]{:S(2)}) async-start(bf16[2,6144,2048]{2,0,1:T(2,128)(2,1)} %copy.44), calls=%async_computation.1 | async-start | bytes 100663296 | tf_op jit(solution)/shard_map/all_to_all | solution.py:48
  1139.2 50.0 %copy-start.3 = (s32[1024,6]{0,1:T(8,128)S(1)}, s32[1024,6]{0,1:T(8,128)}, u32[]{:S(2)}) copy-start(s32[1024,6]{0,1:T(8,128)} %param.10) | copy-start | bytes 73732
  1139.2 50.3 %copy-start.1 = (s32[1024,6]{1,0:T(8,128)S(1)}, s32[1024,6]{1,0:T(8,128)}, u32[]{:S(2)}) copy-start(s32[1024,6]{1,0:T(8,128)} %reduce_sum.50) | copy-start | bytes 73732
  1139.2 50.8 %copy-start.7 = (s32[6144,1]{0,1:T(1,128)S(1)}, s32[6144,1]{0,1:T(1,128)}, u32[]{:S(2)}) copy-start(s32[6144,1]{0,1:T(1,128)} %copy-done.6) | copy-start | bytes 73732
where the time goes:
time: 2050 us; the launch traced here: 2040 us
  waiting for transfers between devices  590 us (29%)
  blocking collectives  553 us (27%)
  local copies, waits for them, and re-layouts  513 us (25%)
  matrix products  270 us (13%)
  other arithmetic  112 us (5%)
    all_to_all x1, waiting for transfers between devices, local_block(): lax.all_to_all(outputs, 'ep', 1, 0, tiled=True)  590 us
    all_to_all x1, blocking collectives, local_block(): received = lax.all_to_all(outgoing, 'ep', 0, 1, tiled=True)  553 us
    gather x2, local copies, waits for them, and re-layouts, local_block(): y_sel = jnp.take(returned, slots, axis=0).reshape(tokens, top_k, hidden)  183 us
    gather x1, local copies, waits for them, and re-layouts, local_block(): jnp.take(normed, slot_tok, axis=0, mode='fill', fill_value=0)  94.1 us
    dot_general x1, matrix products, expert_mlp(): jnp.einsum('erd,edf->erf', rows, w_up, preferred_element_type=jnp.float32)  91.6 us
    convert_element_type x1, local copies, waits for them, and re-layouts, expert_mlp(): jnp.einsum('erf,efd->erd', hidden_act, w_down, preferred_element_type=jnp...  89.5 us
    dot_general x1, matrix products, expert_mlp(): jnp.einsum('erd,edf->erf', rows, w_gate, preferred_element_type=jnp.float32)  87.8 us
    dot_general x1, matrix products, expert_mlp(): jnp.einsum('erf,efd->erd', hidden_act, w_down, preferred_element_type=jnp...  87.3 us
  transfers between devices with their start and end apart: 1, of which 1 were waited for; matrix products, arithmetic and copies ran while one was open for 3% of the time, Pallas kernels for 0%

commit v1 on v0

v1 whole, which is shorter than its diff:
```python
import functools
import math

import jax
import jax.numpy as jnp
from jax import lax
from jax.experimental import pallas as pl
from jax.experimental.pallas import tpu as pltpu
from jax.sharding import PartitionSpec as P

EPS = 1e-6


def norm_rows(x_in, norm_gain):
    resid = x_in.astype(jnp.float32)
    mean_sq = jnp.mean(resid * resid, axis=-1, keepdims=True)
    normed = (resid * lax.rsqrt(mean_sq + EPS) * norm_gain.astype(jnp.float32)).astype(jnp.bfloat16)
    return resid, normed


def choice_weights(normed, w_router, chosen):
    logits = jnp.dot(normed, w_router, preferred_element_type=jnp.float32)
    picked = jnp.where(chosen, jax.nn.softmax(logits, axis=-1), 0.0)
    return picked / jnp.sum(picked, axis=1, keepdims=True)


def split3(value):
    hi = lax.reduce_precision(value, 8, 7)
    rest = value - hi
    mid = lax.reduce_precision(rest, 8, 7)
    low = rest - mid
    return [part.astype(jnp.bfloat16) for part in (hi, mid, low)]


def expert_mlp(rows, w_gate, w_up, w_down):
    gate_val = jnp.dot(rows, w_gate, preferred_element_type=jnp.float32)
    up_val = jnp.dot(rows, w_up, preferred_element_type=jnp.float32)
    hidden_act = (jax.nn.silu(gate_val) * up_val).astype(jnp.bfloat16)
    return jnp.dot(hidden_act, w_down, preferred_element_type=jnp.float32).astype(jnp.bfloat16)


def gather_kernel(group, own_ref, out_ref, send_sems, recv_sems, local_sem):
    side = math.isqrt(group // 2)
    tokens = own_ref.shape[0]
    half, quarter = tokens // 2, tokens // 4
    me = lax.axis_index("ep")
    core, chip = lax.rem(me, 2), me // 2
    here_x, here_y = lax.rem(chip, side), chip // side

    def device(color, a, b):
        dx, dy = (a, b) if color == 0 else (b, a)
        return (lax.rem(here_y + dy + side, side) * side + lax.rem(here_x + dx + side, side)) * 2 + core

    sibling = me + 1 - 2 * core
    barrier = pltpu.get_barrier_semaphore()
    for peer in (device(0, 1, 0), device(0, -1, 0), device(0, 0, 1), device(0, 0, -1), sibling):
        pl.semaphore_signal(barrier, inc=1, device_id={"ep": peer})
    pl.semaphore_wait(barrier, 5)

    counter = iter(range(send_sems.shape[0]))
    slots = {}

    def copy(key, src, start, rows, to, own):
        slot = slots.setdefault(key, None)
        if slot is None:
            slot = slots[key] = next(counter)
        there = out_ref.at[pl.ds(pl.multiple_of(src * tokens + start, quarter), rows)]
        return pltpu.make_async_remote_copy(
            src_ref=own_ref.at[pl.ds(start, rows)] if own else there,
            dst_ref=there,
            send_sem=send_sems.at[slot],
            recv_sem=recv_sems.at[slot],
            device_id={"ep": to},
        )

    sent, awaited = [], []

    def part(color, which):
        start = color * half
        return {"h": (start, half), "q0": (start, quarter), "q1": (start + quarter, quarter)}[which]

    def send(key, src, color, which, to, own=False):
        start, rows = part(color, which)
        dma = copy(key, src, start, rows, to, own)
        dma.start()
        sent.append(dma)

    def arrive(key, src, color, which):
        start, rows = part(color, which)
        copy(key, src, start, rows, me, False).wait_recv()
        send(("sib", *key), src, color, which, sibling)
        awaited.append((("sib", *key), color, which, src))

    colors = (0, 1)
    for color in colors:
        send(("p1", color, 1), me, color, "h", device(color, -1, 0), own=True)
        send(("p1", color, 3), me, color, "h", device(color, 1, 0), own=True)
    for color in colors:
        send(("p2", color, 0, 1), me, color, "h", device(color, 0, -1), own=True)
        send(("p2", color, 0, 3), me, color, "h", device(color, 0, 1), own=True)
    own_copy = pltpu.make_async_copy(own_ref, out_ref.at[pl.ds(pl.multiple_of(me * tokens, tokens), tokens)], local_sem)
    own_copy.start()
    own_to_sibling = copy(("own",), me, 0, tokens, sibling, True)
    own_to_sibling.start()
    sent.append(own_to_sibling)

    def second(color, a):
        src = device(color, a, 0)
        send(("p2", color, a, 1), src, color, "h", device(color, 0, -1))
        send(("p2", color, a, 3), src, color, "h", device(color, 0, 1))

    def second_arrive(color, a):
        arrive(("p2", color, a, 1), device(color, a, 1), color, "h")
        send(("p2", color, a, 2, 0), device(color, a, 1), color, "q0", device(color, 0, -1))
        arrive(("p2", color, a, 3), device(color, a, -1), color, "h")
        send(("p2", color, a, 2, 1), device(color, a, -1), color, "q1", device(color, 0, 1))

    for color in colors:
        arrive(("p1", color, 1), device(color, 1, 0), color, "h")
        send(("p1", color, 2, 0), device(color, 1, 0), color, "q0", device(color, -1, 0))
        arrive(("p1", color, 3), device(color, -1, 0), color, "h")
        send(("p1", color, 2, 1), device(color, -1, 0), color, "q1", device(color, 1, 0))
    for color in colors:
        second(color, 1)
        second(color, -1)
    for color in colors:
        second_arrive(color, 0)
    for color in colors:
        arrive(("p1", color, 2, 0), device(color, 2, 0), color, "q0")
        arrive(("p1", color, 2, 1), device(color, 2, 0), color, "q1")
        second(color, 2)
    for a in (1, -1, 2):
        for color in colors:
            second_arrive(color, a)
    for a in (0, 1, -1, 2):
        for color in colors:
            arrive(("p2", color, a, 2, 0), device(color, a, 2), color, "q0")
            arrive(("p2", color, a, 2, 1), device(color, a, 2), color, "q1")

    other = 1 - 2 * core
    for key, color, which, src in awaited:
        start, rows = part(color, which)
        copy(key, src + other, start, rows, me, False).wait_recv()
    copy(("own",), sibling, 0, tokens, me, False).wait_recv()
    for dma in sent:
        dma.wait_send()
    own_copy.wait()


def gather_rows(rows, group):
    tokens, hidden = rows.shape
    copies = 2 * (4 + 16) * 2 + 1
    return pl.pallas_call(
        functools.partial(gather_kernel, group),
        out_shape=jax.ShapeDtypeStruct((group * tokens, hidden), rows.dtype),
        in_specs=[pl.BlockSpec(memory_space=pltpu.VMEM)],
        out_specs=pl.BlockSpec(memory_space=pl.ANY),
        scratch_shapes=[pltpu.SemaphoreType.DMA((copies,)), pltpu.SemaphoreType.DMA((copies,)), pltpu.SemaphoreType.DMA],
        compiler_params=pltpu.CompilerParams(collective_id=0, has_side_effects=True),
        cost_estimate=pl.CostEstimate(flops=group * tokens * hidden * 1000, bytes_accessed=group * tokens * hidden * 4, transcendentals=0),
        name="gather_rows",
    )(rows)


def solution(mesh):
    group = mesh.shape["ep"]

    def block(x_in, norm_gain, w_router, expert_ids, w_gate, w_up, w_down):
        tokens, hidden = x_in.shape
        experts = w_router.shape[1]
        top_k = expert_ids.shape[1]
        held = w_gate.shape[0]
        capacity = 2 * tokens * top_k // experts
        slot_range = jnp.arange(capacity, dtype=jnp.int32)

        chosen = jnp.any(expert_ids[:, :, None] == jnp.arange(experts, dtype=jnp.int32), axis=1)
        place = jnp.where(chosen, jnp.cumsum(chosen.astype(jnp.int32), axis=0) - 1, -1)
        at_slot = place.T[:, None, :] == slot_range[None, :, None]
        slot_tok = jnp.sum(jnp.where(at_slot, jnp.arange(tokens, dtype=jnp.int32), 0), axis=-1)
        slot_row = slot_tok + tokens * lax.axis_index("ep")
        src_row = lax.all_to_all(slot_row.reshape(group, held, capacity), "ep", 0, 0, tiled=True)

        resid, normed = norm_rows(x_in, norm_gain)
        all_rows = gather_rows(normed, group)
        weight = choice_weights(normed, w_router, chosen)

        third = capacity // 3
        cuts = [((0, third), (third, capacity)) if e == 0 else ((0, capacity - third), (capacity - third, capacity)) for e in range(held)]
        pieces = [(e, lo, hi) for e in range(held) for lo, hi in cuts[e]]
        mixed = resid
        out_rows = None
        for k, (e, lo, hi) in enumerate(pieces):
            if k:
                src_row, out_rows = lax.optimization_barrier((src_row, out_rows))
            rows = jnp.take(all_rows, src_row[:, e, lo:hi].reshape(-1), axis=0, mode="clip")
            out_rows = expert_mlp(rows, w_gate[e], w_up[e], w_down[e])
            if k == 0:
                place, weight, _ = lax.optimization_barrier((place, weight, out_rows))
            back = lax.all_to_all(out_rows.reshape(group, hi - lo, hidden), "ep", 0, 0, tiled=True)
            back = back.reshape(group * (hi - lo), hidden)
            mix = jnp.where(
                place.reshape(tokens, group, held)[:, :, e, None] == slot_range[lo:hi],
                weight.reshape(tokens, group, held)[:, :, e, None],
                0.0,
            )
            parts = lax.optimization_barrier(split3(mix.reshape(tokens, group * (hi - lo))))
            for part in parts:
                mixed = mixed + jnp.dot(part, back, preferred_element_type=jnp.float32)
            if k < len(pieces) - 1:
                mixed = lax.optimization_barrier(mixed)
        return mixed.astype(jnp.bfloat16)

    tok_spec = P(("dp", "ep"), None)
    expert_spec = P("ep", None, None)
    return jax.shard_map(block, mesh=mesh, in_specs=(tok_spec, P(None), P(None, None), tok_spec, expert_spec, expert_spec, expert_spec), out_specs=tok_spec, check_vma=False)
```

time: 2050 us -> 2040 us (level)
  the two profiles are of different devices: /device:TPU:96 before, /device:TPU:123 now
where the time goes in v1:
time: 2040 us; the launch traced here: 2010 us
  local copies, waits for them, and re-layouts  606 us (30%)
  matrix products  559 us (27%)
  Pallas kernels  352 us (17%)
  waiting for transfers between devices  251 us (12%)
  blocking collectives  98.7 us (5%)
  other arithmetic  94 us (5%)
  starting transfers between devices  45.4 us (2%)
    gather x4, local copies, waits for them, and re-layouts, block(): jnp.take(all_rows, src_row[:, e, lo:hi].reshape(-1), axis=0, mode='clip')  565 us
    pallas_call x1, Pallas kernels, gather_rows(): pl.pallas_call(functools.partial(gather_kernel, group), out_shape=jax.Sha...  352 us
    all_to_all x3, waiting for transfers between devices, block(): lax.all_to_all(out_rows.reshape(group, hi - lo, hidden), 'ep', 0, 0, tile...  251 us
    dot_general x12, matrix products, block(): mixed = mixed + jnp.dot(part, back, preferred_element_type=jnp.float32)  243 us
    dot_general x4, matrix products, expert_mlp(): jnp.dot(hidden_act, w_down, preferred_element_type=jnp.float32)  135 us
    dot_general x4, matrix products, expert_mlp(): gate_val = jnp.dot(rows, w_gate, preferred_element_type=jnp.float32)  103 us
    all_to_all x1, blocking collectives, block(): lax.all_to_all(out_rows.reshape(group, hi - lo, hidden), 'ep', 0, 0, tile...  98.7 us
    dot_general x2, matrix products, expert_mlp(): up_val = jnp.dot(rows, w_up, preferred_element_type=jnp.float32)  74.2 us
  transfers between devices with their start and end apart: 4, of which 3 were waited for; matrix products, arithmetic and copies ran while one was open for 13% of the time, Pallas kernels for 18%

profile of v1, /device:TPU:123, one launch (start us, length us, event | category | flops | bytes accessed | tf_op | source)
XLA Modules:
  0.0 2007.4 jit_solution(16713700127421468294)
XLA Ops:
  43.5 352.2 %gather_rows.1 = bf16[32768,2048]{1,0:T(8,128)(2,1)} custom-call(bf16[1024,2048]{1,0:T(8,128)(2,1)} %fusion.6.own_ref), custom_call_target="tpu_custom_call" | custom-call | flops 67108864000 | bytes 268435456 | tf_op jit(solution)/shard_map/gather_rows/pallas_call | solution.py:153
  395.9 48.1 %gather_fusion = bf16[2048,2048]{1,0:T(8,128)(2,1)} fusion(bf16[32768,2048]{1,0:T(8,128)(2,1)} %gather_rows.1, s32[2048]{0:T(1024)S(1)} %broadcast_clamp_fusion.3), kind=kCustom, calls=%fused_computation | custom fusion | bytes 16785408 | tf_op jit(solution)/shard_map/jit(_take)/gather | solution.py:195
  462.6 35.5 %convolution_convert_fusion.3 = bf16[2048,2048]{1,0:T(8,128)(2,1)} fusion(f32[2048,1408]{1,0:T(8,128)} %fusion.27, bf16[2048,2048]{1,0:T(8,128)(2,1)} %gather_fusion, bf16[2,1408,2048]{2,1,0:T(8,128)(2,1)} %param.13, bf16[2,2048,1408]{2,1,0:T(8,128)(2,1)} %param.12), kind=kOutput, calls=%fused_computation.52 | convolution fusion | flops 23643815936 | bytes 39845888 | tf_op jit(solution)/shard_map/dot_general | solution.py:39
  498.2 254.2 %gather_fusion.1 = bf16[4096,2048]{1,0:T(8,128)(2,1)} fusion(bf16[32768,2048]{1,0:T(8,128)(2,1)} %gather_rows.1, s32[4096]{0:T(1024)S(1)} %broadcast_clamp_fusion.1), kind=kCustom, calls=%fused_computation.1 | custom fusion | bytes 33570816 | tf_op jit(solution)/shard_map/jit(_take)/gather | solution.py:195
  752.4 33.0 %fusion.25 = f32[4096,1408]{1,0:T(8,128)} fusion(bf16[4096,2048]{1,0:T(8,128)(2,1)} %gather_fusion.1, bf16[2,2048,1408]{2,1,0:T(8,128)(2,1)} %param.11), kind=kOutput, calls=%fused_computation.65 | convolution fusion | flops 23622320128 | bytes 45613056 | tf_op jit(solution)/shard_map/dot_general | solution.py:36
  785.4 37.2 %multiply_convert_fusion.1.clone.5 = bf16[4096,1408]{1,0:T(8,128)(2,1)} fusion(f32[4096,1408]{1,0:T(8,128)} %fusion.25, bf16[4096,2048]{1,0:T(8,128)(2,1)} %gather_fusion.1, bf16[2,2048,1408]{2,1,0:T(8,128)(2,1)} %param.12), kind=kOutput, calls=%fused_computation.15.clone.clone.clone.2 | convolution fusion | flops 23656923136 | bytes 57147392 | tf_op jit(solution)/shard_map/dot_general | solution.py:37
  822.6 32.1 %convolution_convert_fusion.1 = bf16[4096,2048]{1,0:T(8,128)(2,1)} fusion(bf16[2,1408,2048]{2,1,0:T(8,128)(2,1)} %param.13, bf16[4096,1408]{1,0:T(8,128)(2,1)} %multiply_convert_fusion.1.clone.5), kind=kOutput, calls=%fused_computation.23 | convolution fusion | flops 23630708736 | bytes 34078720 | tf_op jit(solution)/shard_map/dot_general | solution.py:39
  855.5 172.3 %gather_fusion.2 = bf16[4096,2048]{1,0:T(8,128)(2,1)} fusion(bf16[32768,2048]{1,0:T(8,128)(2,1)} %gather_rows.1, s32[4096]{0:T(1024)S(1)} %broadcast_clamp_fusion), kind=kCustom, calls=%fused_computation.2 | custom fusion | bytes 33570816 | tf_op jit(solution)/shard_map/jit(_take)/gather | solution.py:195
  1027.8 33.0 %fusion.17 = f32[4096,1408]{1,0:T(8,128)} fusion(bf16[4096,2048]{1,0:T(8,128)(2,1)} %gather_fusion.2, bf16[2,2048,1408]{2,1,0:T(8,128)(2,1)} %param.11), kind=kOutput, calls=%fused_computation.59 | convolution fusion | flops 23622320128 | bytes 45613056 | tf_op jit(solution)/shard_map/dot_general | solution.py:36
  1060.8 37.0 %multiply_convert_fusion.clone.5 = bf16[4096,1408]{1,0:T(8,128)(2,1)} fusion(f32[4096,1408]{1,0:T(8,128)} %fusion.17, bf16[4096,2048]{1,0:T(8,128)(2,1)} %gather_fusion.2, bf16[2,2048,1408]{2,1,0:T(8,128)(2,1)} %param.12), kind=kOutput, calls=%fused_computation.14.clone.clone.clone.2 | convolution fusion | flops 23656923136 | bytes 57147392 | tf_op jit(solution)/shard_map/dot_general | solution.py:37
  1097.8 32.1 %convolution_convert_fusion = bf16[4096,2048]{1,0:T(8,128)(2,1)} fusion(bf16[2,1408,2048]{2,1,0:T(8,128)(2,1)} %param.13, bf16[4096,1408]{1,0:T(8,128)(2,1)} %multiply_convert_fusion.clone.5), kind=kOutput, calls=%fused_computation.22 | convolution fusion | flops 23630708736 | bytes 34078720 | tf_op jit(solution)/shard_map/dot_general | solution.py:39
  1130.8 90.8 %gather_fusion.3 = bf16[2048,2048]{1,0:T(8,128)(2,1)} fusion(bf16[32768,2048]{1,0:T(8,128)(2,1)} %gather_rows.1, s32[2048]{0:T(1024)S(1)} %broadcast_clamp_fusion.2), kind=kCustom, calls=%fused_computation.3 | custom fusion | bytes 16785408 | tf_op jit(solution)/shard_map/jit(_take)/gather | solution.py:195
  1240.2 35.1 %convolution_convert_fusion.2 = bf16[2048,2048]{1,0:T(8,128)(2,1)} fusion(f32[2048,1408]{1,0:T(8,128)} %fusion.15, bf16[2048,2048]{1,0:T(8,128)(2,1)} %gather_fusion.3, bf16[2,1408,2048]{2,1,0:T(8,128)(2,1)} %param.13, bf16[2,2048,1408]{2,1,0:T(8,128)(2,1)} %param.12), kind=kOutput, calls=%fused_computation.51 | convolution fusion | flops 23643815936 | bytes 39845888 | tf_op jit(solution)/shard_map/dot_general | solution.py:39
  1275.3 98.7 %all_to_all.25 = bf16[32,64,2048]{2,1,0:T(8,128)(2,1)} all-to-all(bf16[32,64,2048]{2,1,0:T(8,128)(2,1)} %bitcast.205), channel_id=1, replica_groups=mesh['dp'=1,'ep'=32] {'ep'}, dimensions={0} | all-to-all | bytes 16777216 | tf_op jit(solution)/shard_map/all_to_all | solution.py:199
  1385.1 94.6 %all-to-all-done.1 = bf16[32,64,2048]{2,1,0:T(8,128)(2,1)} async-done(((bf16[32,64,2048]{2,1,0:T(8,128)(2,1)}), bf16[32,64,2048]{2,1,0:T(8,128)(2,1)}, u32[]{:S(2)}, u32[]{:S(2)}) %all-to-all-start.1) | async-done | bytes 8388640 | tf_op jit(solution)/shard_map/all_to_all | solution.py:199
  1634.6 57.7 %all-to-all-done.2 = bf16[32,128,2048]{2,1,0:T(8,128)(2,1)} async-done(((bf16[32,128,2048]{2,1,0:T(8,128)(2,1)}), bf16[32,128,2048]{2,1,0:T(8,128)(2,1)}, u32[]{:S(2)}, u32[]{:S(2)}) %all-to-all-start.2) | async-done | bytes 16777248 | tf_op jit(solution)/shard_map/all_to_all | solution.py:199
  1739.3 21.6 %fusion.61 = f32[1024,2048]{1,0:T(8,128)} fusion(bf16[1024,4096]{1,0:T(8,128)(2,1)S(1)} %bitcast.209, bf16[4096,2048]{1,0:T(8,128)(2,1)} %bitcast.13), kind=kOutput, calls=%fused_computation.119 | convolution fusion | flops 17179869184 | bytes 33554432 | tf_op jit(solution)/shard_map/dot_general | solution.py:208
  1760.9 21.7 %fusion.60 = f32[1024,2048]{1,0:T(8,128)} fusion(bf16[1024,4096]{1,0:T(8,128)(2,1)S(1)} %bitcast.207, bf16[4096,2048]{1,0:T(8,128)(2,1)} %bitcast.13), kind=kOutput, calls=%fused_computation.118 | convolution fusion | flops 17179869184 | bytes 33554432 | tf_op jit(solution)/shard_map/dot_general | solution.py:208
  1782.6 28.9 %add_add_fusion.1 = f32[1024,2048]{1,0:T(8,128)} fusion(f32[1024,2048]{1,0:T(8,128)} %fusion.61, f32[1024,2048]{1,0:T(8,128)} %fusion.8, f32[1024,2048]{1,0:T(8,128)} %fusion.60, bf16[1024,4096]{1,0:T(8,128)(2,1)} %get-tuple-element.30, bf16[4096,2048]{1,0:T(8,128)(2,1)} %bitcast.13), kind=kOutput, calls=%fused_computation.50 | convolution fusion | flops 17186160640 | bytes 58720256 | tf_op jit(solution)/shard_map/dot_general | solution.py:208
  1811.4 99.1 %all-to-all-done.3 = bf16[32,128,2048]{2,1,0:T(8,128)(2,1)} async-done(((bf16[32,128,2048]{2,1,0:T(8,128)(2,1)}), bf16[32,128,2048]{2,1,0:T(8,128)(2,1)}, u32[]{:S(2)}, u32[]{:S(2)}) %all-to-all-start.3) | async-done | bytes 16777248 | tf_op jit(solution)/shard_map/all_to_all | solution.py:199
  1910.5 24.0 %fusion.63 = f32[1024,2048]{1,0:T(8,128)} fusion(bf16[1024,4096]{1,0:T(8,128)(2,1)} %get-tuple-element.33, bf16[4096,2048]{1,0:T(8,128)(2,1)} %bitcast.20), kind=kOutput, calls=%fused_computation.121 | convolution fusion | flops 17179869184 | bytes 33554432 | tf_op jit(solution)/shard_map/dot_general | solution.py:208
  1934.5 24.2 %fusion.62 = f32[1024,2048]{1,0:T(8,128)} fusion(bf16[1024,4096]{1,0:T(8,128)(2,1)} %get-tuple-element.31, bf16[4096,2048]{1,0:T(8,128)(2,1)} %bitcast.20), kind=kOutput, calls=%fused_computation.120 | convolution fusion | flops 17179869184 | bytes 33554432 | tf_op jit(solution)/shard_map/dot_general | solution.py:208
  1958.7 28.9 %add_add_fusion = f32[1024,2048]{1,0:T(8,128)} fusion(f32[1024,2048]{1,0:T(8,128)} %fusion.63, f32[1024,2048]{1,0:T(8,128)} %add_add_fusion.1, f32[1024,2048]{1,0:T(8,128)} %fusion.62, bf16[1024,4096]{1,0:T(8,128)(2,1)} %get-tuple-element.34, bf16[4096,2048]{1,0:T(8,128)(2,1)} %bitcast.20), kind=kOutput, calls=%fused_computation.49 | convolution fusion | flops 17186160640 | bytes 58720256 | tf_op jit(solution)/shard_map/dot_general | solution.py:208
  1987.6 19.5 add_convert_fusion
  (107 shorter events, 295.1 us)
Async XLA Ops:
  0.0 1381.4 %copy-start = (bf16[2048,64]{0,1:T(8,128)(2,1)S(1)}, bf16[2048,64]{0,1:T(8,128)(2,1)}, u32[]{:S(2)}) copy-start(bf16[2048,64]{0,1:T(8,128)(2,1)} %param.9) | copy-start | bytes 786436
  1.0 394.8 %copy-start.4 = (pred[1024,64]{0,1:T(8,128)(4,1)}, pred[1024,64]{0,1:T(8,128)(4,1)S(1)}, u32[]{:S(2)}) copy-start(pred[1024,64]{0,1:T(8,128)(4,1)S(1)} %fusion.47) | copy-start | bytes 196612
  19.7 0.7 copy-start.6
  27.1 368.7 %all-to-all-start = ((s32[32,2,192]{2,1,0:T(2,128)}), s32[32,2,192]{2,1,0:T(2,128)S(1)}, u32[]{:S(2)}, u32[]{:S(2)}) async-start(s32[32,2,192]{2,1,0:T(2,128)} %add.80), calls=%async_computation | async-start | bytes 131072 | tf_op jit(solution)/shard_map/all_to_all | solution.py:181
  395.8 102.3 %copy-start.8 = (s32[32,2,192]{2,1,0:T(2,128)}, s32[32,2,192]{2,1,0:T(2,128)S(1)}, u32[]{:S(2)}) copy-start(s32[32,2,192]{2,1,0:T(2,128)S(1)} %all-to-all-done) | copy-start | bytes 147460
  1374.0 11.0 copy-start.5
  1374.0 11.0 copy-start.7
  1374.0 105.7 %all-to-all-start.1 = ((bf16[32,64,2048]{2,1,0:T(8,128)(2,1)}), bf16[32,64,2048]{2,1,0:T(8,128)(2,1)}, u32[]{:S(2)}, u32[]{:S(2)}) async-start(bf16[32,64,2048]{2,1,0:T(8,128)(2,1)} %bitcast.204), calls=%async_computation.1 | async-start | bytes 16777216 | tf_op jit(solution)/shard_map/all_to_all | solution.py:199
  1479.8 212.6 %all-to-all-start.2 = ((bf16[32,128,2048]{2,1,0:T(8,128)(2,1)}), bf16[32,128,2048]{2,1,0:T(8,128)(2,1)}, u32[]{:S(2)}, u32[]{:S(2)}) async-start(bf16[32,128,2048]{2,1,0:T(8,128)(2,1)} %bitcast.200), calls=%async_computation.2 | async-start | bytes 33554432 | tf_op jit(solution)/shard_map/all_to_all | solution.py:199
  1602.8 14.0 copy-start.1
  1692.3 218.2 %all-to-all-start.3 = ((bf16[32,128,2048]{2,1,0:T(8,128)(2,1)}), bf16[32,128,2048]{2,1,0:T(8,128)(2,1)}, u32[]{:S(2)}, u32[]{:S(2)}) async-start(bf16[32,128,2048]{2,1,0:T(8,128)(2,1)} %bitcast.199), calls=%async_computation.3 | async-start | bytes 33554432 | tf_op jit(solution)/shard_map/all_to_all | solution.py:199
  1710.5 14.9 copy-start.3
  1710.6 28.7 %slice-start.2 = ((s8[8388608]{0:T(1024)(128)(4,1)}), s8[4194304]{0:T(1024)(128)(4,1)S(1)}, s32[]{:S(2)}) async-start(s8[8388608]{0:T(1024)(128)(4,1)} %bitcast.208), calls=%async_computation.7 | async-start | bytes 8388608
  1725.4 13.8 slice-start.3
  1725.4 35.4 %slice-start = ((s8[8388608]{0:T(1024)(128)(4,1)}), s8[4194304]{0:T(1024)(128)(4,1)S(1)}, s32[]{:S(2)}) async-start(s8[8388608]{0:T(1024)(128)(4,1)} %bitcast.206), calls=%async_computation.5 | async-start | bytes 8388608
  1739.3 21.6 %slice-start.1 = ((s8[8388608]{0:T(1024)(128)(4,1)}), s8[4194304]{0:T(1024)(128)(4,1)S(1)}, s32[]{:S(2)}) async-start(s8[8388608]{0:T(1024)(128)(4,1)} %bitcast.206), calls=%async_computation.6 | async-start | bytes 8388608
  1958.7 28.9 %copy-start.2 = (bf16[1024,2048]{0,1:T(8,128)(2,1)S(1)}, bf16[1024,2048]{0,1:T(8,128)(2,1)}, u32[]{:S(2)}) copy-start(bf16[1024,2048]{0,1:T(8,128)(2,1)} %get-tuple-element.38) | copy-start | bytes 12582916

commit v2 on v1

--- a/solution.py
+++ b/solution.py
@@ -162,6 +162,35 @@
     )(rows)
 
 
+def pick_kernel(bounds, tok_ref, rows_ref, *out_refs):
+    tokens, hidden = rows_ref.shape[1:]
+    slots = tok_ref.shape[2]
+    lanes = min(128, tokens)
+    column = jnp.broadcast_to(tok_ref[0], (lanes, slots)).T
+    lane = lax.broadcasted_iota(jnp.int32, (slots, lanes), 1)
+    pick = jnp.concatenate([jnp.where(column == lane + start, 1.0, 0.0).astype(jnp.bfloat16) for start in range(0, tokens, lanes)], axis=1)
+    width = hidden // 4
+    for start in range(0, hidden, width):
+        rows = jnp.dot(pick, rows_ref[0, :, start : start + width], preferred_element_type=jnp.float32).astype(jnp.bfloat16)
+        for out_ref, (lo, hi) in zip(out_refs, bounds):
+            out_ref[0, :, start : start + width] = rows[lo:hi]
+
+
+def pick_rows(src_tok, all_rows, bounds):
+    group, tokens, hidden = all_rows.shape
+    slots = src_tok.shape[2]
+    return pl.pallas_call(
+        functools.partial(pick_kernel, bounds),
+        grid=(group,),
+        out_shape=[jax.ShapeDtypeStruct((group, hi - lo, hidden), all_rows.dtype) for lo, hi in bounds],
+        in_specs=[pl.BlockSpec((1, 1, slots), lambda s: (s, 0, 0)), pl.BlockSpec((1, tokens, hidden), lambda s: (s, 0, 0))],
+        out_specs=[pl.BlockSpec((1, hi - lo, hidden), lambda s: (s, 0, 0)) for lo, hi in bounds],
+        compiler_params=pltpu.CompilerParams(vmem_limit_bytes=48 * 1024 * 1024),
+        cost_estimate=pl.CostEstimate(flops=2 * group * slots * tokens * hidden, bytes_accessed=2 * group * (tokens + slots) * hidden, transcendentals=0),
+        name="pick_rows",
+    )(src_tok, all_rows)
+
+
 def solution(mesh):
     group = mesh.shape["ep"]
 
@@ -174,25 +203,28 @@
         slot_range = jnp.arange(capacity, dtype=jnp.int32)
 
         chosen = jnp.any(expert_ids[:, :, None] == jnp.arange(experts, dtype=jnp.int32), axis=1)
-        place = jnp.where(chosen, jnp.cumsum(chosen.astype(jnp.int32), axis=0) - 1, -1)
+        earlier = jnp.arange(tokens)[:, None] >= jnp.arange(tokens)[None, :]
+        count = jnp.dot(earlier.astype(jnp.bfloat16), chosen.astype(jnp.bfloat16), preferred_element_type=jnp.float32)
+        place = jnp.where(chosen, count.astype(jnp.int32) - 1, -1)
         at_slot = place.T[:, None, :] == slot_range[None, :, None]
-        slot_tok = jnp.sum(jnp.where(at_slot, jnp.arange(tokens, dtype=jnp.int32), 0), axis=-1)
-        slot_row = slot_tok + tokens * lax.axis_index("ep")
-        src_row = lax.all_to_all(slot_row.reshape(group, held, capacity), "ep", 0, 0, tiled=True)
+        slot_tok = jnp.sum(jnp.where(at_slot, jnp.arange(1, tokens + 1, dtype=jnp.int32), 0), axis=-1) - 1
+        src_tok = lax.all_to_all(slot_tok.reshape(group, held, capacity), "ep", 0, 0, tiled=True)
 
         resid, normed = norm_rows(x_in, norm_gain)
-        all_rows = gather_rows(normed, group)
+        all_rows = gather_rows(normed, group).reshape(group, tokens, hidden)
         weight = choice_weights(normed, w_router, chosen)
 
         third = capacity // 3
         cuts = [((0, third), (third, capacity)) if e == 0 else ((0, capacity - third), (capacity - third, capacity)) for e in range(held)]
         pieces = [(e, lo, hi) for e in range(held) for lo, hi in cuts[e]]
+        bounds = tuple((e * capacity + lo, e * capacity + hi) for e, lo, hi in pieces)
+        piece_rows = pick_rows(src_tok.reshape(group, 1, held * capacity), all_rows, bounds)
         mixed = resid
         out_rows = None
         for k, (e, lo, hi) in enumerate(pieces):
+            rows = piece_rows[k].reshape(group * (hi - lo), hidden)
             if k:
-                src_row, out_rows = lax.optimization_barrier((src_row, out_rows))
-            rows = jnp.take(all_rows, src_row[:, e, lo:hi].reshape(-1), axis=0, mode="clip")
+                rows, out_rows = lax.optimization_barrier((rows, out_rows))
             out_rows = expert_mlp(rows, w_gate[e], w_up[e], w_down[e])
             if k == 0:
                 place, weight, _ = lax.optimization_barrier((place, weight, out_rows))

time: 2040 us -> 1480 us (0.73)
  local copies, waits for them, and re-layouts: 606 us -> 38.9 us
  blocking collectives: 98.7 us -> 0 us
  Pallas kernels: 352 us -> 429 us
  waiting for transfers between devices: 251 us -> 296 us
    gather x4 -> x0, local copies, waits for them, and re-layouts: 565 us -> none  [block(): jnp.take(all_rows, src_row[:, e, lo:hi].reshape(-1), axis=0, mode='clip')]
    all_to_all x1 -> x0, blocking collectives: 98.7 us -> none  [block(): lax.all_to_all(out_rows.reshape(group, hi - lo, hidden), 'ep', 0, 0, tile...]
    pallas_call x0 -> x1, Pallas kernels: none -> 76.9 us  [pick_rows(): pl.pallas_call(functools.partial(pick_kernel, bounds), grid=(group,), out...]
    all_to_all x3 -> x4, waiting for transfers between devices: 251 us -> 296 us  [block(): lax.all_to_all(out_rows.reshape(group, hi - lo, hidden), 'ep', 0, 0, tile...]
    all_to_all x3 -> x4, starting transfers between devices: 38 us -> 47.7 us  [block(): lax.all_to_all(out_rows.reshape(group, hi - lo, hidden), 'ep', 0, 0, tile...]
  transfers between devices with their start and end apart: 4 -> 5, of which waited for: 3 -> 4; matrix products, arithmetic and copies ran while one was open for 13% -> 21% of each run, Pallas kernels for 18% -> 24%
where the time goes in v2:
time: 1480 us; the launch traced here: 1450 us
  matrix products  558 us (38%)
  Pallas kernels  429 us (29%)
  waiting for transfers between devices  296 us (20%)
  other arithmetic  76.2 us (5%)
  starting transfers between devices  54.9 us (4%)
  local copies, waits for them, and re-layouts  38.9 us (3%)
    pallas_call x1, Pallas kernels, gather_rows(): pl.pallas_call(functools.partial(gather_kernel, group), out_shape=jax.Sha...  352 us
    all_to_all x4, waiting for transfers between devices, block(): lax.all_to_all(out_rows.reshape(group, hi - lo, hidden), 'ep', 0, 0, tile...  296 us
    dot_general x12, matrix products, block(): mixed = mixed + jnp.dot(part, back, preferred_element_type=jnp.float32)  243 us
    dot_general x4, matrix products, expert_mlp(): jnp.dot(hidden_act, w_down, preferred_element_type=jnp.float32)  135 us
    dot_general x4, matrix products, expert_mlp(): gate_val = jnp.dot(rows, w_gate, preferred_element_type=jnp.float32)  102 us
    pallas_call x1, Pallas kernels, pick_rows(): pl.pallas_call(functools.partial(pick_kernel, bounds), grid=(group,), out...  76.9 us
    dot_general x2, matrix products, expert_mlp(): up_val = jnp.dot(rows, w_up, preferred_element_type=jnp.float32)  74.1 us
    convert_element_type x6, other arithmetic, split3(): return [part.astype(jnp.bfloat16) for part in (hi, mid, low)]  60 us
  transfers between devices with their start and end apart: 5, of which 4 were waited for; matrix products, arithmetic and copies ran while one was open for 21% of the time, Pallas kernels for 24%

profile of v2, /device:TPU:123, one launch (start us, length us, event | category | flops | bytes accessed | tf_op | source)
XLA Modules:
  0.0 1454.0 jit_solution(2893139807804679977)
XLA Ops:
  25.1 352.2 %gather_rows.1 = bf16[32768,2048]{1,0:T(8,128)(2,1)} custom-call(bf16[1024,2048]{1,0:T(8,128)(2,1)} %fusion.6.own_ref), custom_call_target="tpu_custom_call" | custom-call | flops 67108864000 | bytes 268435456 | tf_op jit(solution)/shard_map/gather_rows/pallas_call | solution.py:153
  377.6 76.9 %pick_rows.1 = (bf16[32,64,2048]{2,1,0:T(8,128)(2,1)}, bf16[32,128,2048]{2,1,0:T(8,128)(2,1)}, bf16[32,128,2048]{2,1,0:T(8,128)(2,1)}, bf16[32,64,2048]{2,1,0:T(8,128)(2,1)}) custom-call(s32[32,1,384]{2,1,0:T(1,128)S(1)} %reshape.92.tok_ref, bf16[32,1024,2048]{2,1,0:T(8,128)(2,1)} %bitcast.1.rows_ref), custom_call_target="tpu_custom_call" | custom-call | flops 51539607552 | bytes 184549376 | tf_op jit(solution)/shard_map/pick_rows/pallas_call | solution.py:182
  454.5 18.5 %fusion.27 = f32[2048,1408]{1,0:T(8,128)} fusion(bf16[2048,2048]{1,0:T(8,128)(2,1)} %bitcast.206, bf16[2,2048,1408]{2,1,0:T(8,128)(2,1)} %param.11), kind=kOutput, calls=%fused_computation.63 | convolution fusion | flops 11811160064 | bytes 25690112 | tf_op jit(solution)/shard_map/dot_general | solution.py:36
  473.0 35.4 %convolution_convert_fusion.3 = bf16[2048,2048]{1,0:T(8,128)(2,1)} fusion(f32[2048,1408]{1,0:T(8,128)} %fusion.27, bf16[2048,2048]{1,0:T(8,128)(2,1)} %bitcast.207, bf16[2,1408,2048]{2,1,0:T(8,128)(2,1)} %param.13, bf16[2,2048,1408]{2,1,0:T(8,128)(2,1)} %param.12), kind=kOutput, calls=%fused_computation.48 | convolution fusion | flops 23643815936 | bytes 39845888 | tf_op jit(solution)/shard_map/dot_general | solution.py:39
  508.4 33.0 %fusion.25 = f32[4096,1408]{1,0:T(8,128)} fusion(bf16[4096,2048]{1,0:T(8,128)(2,1)} %bitcast.202, bf16[2,2048,1408]{2,1,0:T(8,128)(2,1)} %param.11), kind=kOutput, calls=%fused_computation.61 | convolution fusion | flops 23622320128 | bytes 45613056 | tf_op jit(solution)/shard_map/dot_general | solution.py:36
  541.4 37.3 %multiply_convert_fusion.1.clone.5 = bf16[4096,1408]{1,0:T(8,128)(2,1)} fusion(f32[4096,1408]{1,0:T(8,128)} %fusion.25, bf16[4096,2048]{1,0:T(8,128)(2,1)} %bitcast.203, bf16[2,2048,1408]{2,1,0:T(8,128)(2,1)} %param.12), kind=kOutput, calls=%fused_computation.11.clone.clone.clone.2 | convolution fusion | flops 23656923136 | bytes 57147392 | tf_op jit(solution)/shard_map/dot_general | solution.py:37
  578.7 32.3 %convolution_convert_fusion.1 = bf16[4096,2048]{1,0:T(8,128)(2,1)} fusion(bf16[2,1408,2048]{2,1,0:T(8,128)(2,1)} %param.13, bf16[4096,1408]{1,0:T(8,128)(2,1)} %multiply_convert_fusion.1.clone.5), kind=kOutput, calls=%fused_computation.19 | convolution fusion | flops 23630708736 | bytes 34078720 | tf_op jit(solution)/shard_map/dot_general | solution.py:39
  611.0 31.5 %fusion.17 = f32[4096,1408]{1,0:T(8,128)} fusion(bf16[4096,2048]{1,0:T(8,128)(2,1)} %bitcast.200, bf16[2,2048,1408]{2,1,0:T(8,128)(2,1)S(1)} %copy-done.8), kind=kOutput, calls=%fused_computation.55 | convolution fusion | flops 23622320128 | bytes 45613056 | tf_op jit(solution)/shard_map/dot_general | solution.py:36
  642.5 36.8 %multiply_convert_fusion.clone.5 = bf16[4096,1408]{1,0:T(8,128)(2,1)} fusion(f32[4096,1408]{1,0:T(8,128)} %fusion.17, bf16[4096,2048]{1,0:T(8,128)(2,1)} %bitcast.201, bf16[2,2048,1408]{2,1,0:T(8,128)(2,1)} %param.12), kind=kOutput, calls=%fused_computation.10.clone.clone.clone.2 | convolution fusion | flops 23656923136 | bytes 57147392 | tf_op jit(solution)/shard_map/dot_general | solution.py:37
  679.3 32.5 %convolution_convert_fusion = bf16[4096,2048]{1,0:T(8,128)(2,1)} fusion(bf16[2,1408,2048]{2,1,0:T(8,128)(2,1)} %param.13, bf16[4096,1408]{1,0:T(8,128)(2,1)} %multiply_convert_fusion.clone.5), kind=kOutput, calls=%fused_computation.18 | convolution fusion | flops 23630708736 | bytes 34078720 | tf_op jit(solution)/shard_map/dot_general | solution.py:39
  736.3 35.1 %convolution_convert_fusion.2 = bf16[2048,2048]{1,0:T(8,128)(2,1)} fusion(f32[2048,1408]{1,0:T(8,128)} %fusion.15, bf16[2048,2048]{1,0:T(8,128)(2,1)} %bitcast.205, bf16[2,1408,2048]{2,1,0:T(8,128)(2,1)} %param.13, bf16[2,2048,1408]{2,1,0:T(8,128)(2,1)} %param.12), kind=kOutput, calls=%fused_computation.47 | convolution fusion | flops 23643815936 | bytes 39845888 | tf_op jit(solution)/shard_map/dot_general | solution.py:39
  771.4 45.2 %all-to-all-done.1 = bf16[32,64,2048]{2,1,0:T(8,128)(2,1)} async-done(((bf16[32,64,2048]{2,1,0:T(8,128)(2,1)}), bf16[32,64,2048]{2,1,0:T(8,128)(2,1)}, u32[]{:S(2)}, u32[]{:S(2)}) %all-to-all-start.1) | async-done | bytes 8388640 | tf_op jit(solution)/shard_map/all_to_all | solution.py:231
  831.6 94.7 %all-to-all-done.4 = bf16[32,64,2048]{2,1,0:T(8,128)(2,1)} async-done(((bf16[32,64,2048]{2,1,0:T(8,128)(2,1)}), bf16[32,64,2048]{2,1,0:T(8,128)(2,1)}, u32[]{:S(2)}, u32[]{:S(2)}) %all-to-all-start.4) | async-done | bytes 8388640 | tf_op jit(solution)/shard_map/all_to_all | solution.py:231
  958.2 19.1 %fusion.1 = (bf16[1024,4096]{1,0:T(8,128)(2,1)}, f32[1024,4096]{1,0:T(8,128)S(1)}) fusion(f32[128,8,32,128]{3,2,1,0:T(8,128)} %bitcast.185, s32[4096]{0:T(1024)S(1)} %broadcast_bitcast_fusion, s32[128,8,32,128]{3,2,1,0:T(8,128)} %bitcast.183), kind=kLoop, calls=%fused_computation.13 | loop fusion | flops 29360128 | bytes 58736640 | tf_op jit(solution)/shard_map/convert_element_type | solution.py:32
  1002.4 19.0 %fusion = (bf16[1024,4096]{1,0:T(8,128)(2,1)}, f32[1024,4096]{1,0:T(8,128)S(1)}) fusion(f32[128,8,32,128]{3,2,1,0:T(8,128)} %bitcast.186, s32[4096]{0:T(1024)S(1)} %broadcast_bitcast_fusion.1, s32[128,8,32,128]{3,2,1,0:T(8,128)} %bitcast.184), kind=kLoop, calls=%fused_computation.12 | loop fusion | flops 29360128 | bytes 58736640 | tf_op jit(solution)/shard_map/convert_element_type | solution.py:32
  1081.6 57.3 %all-to-all-done.2 = bf16[32,128,2048]{2,1,0:T(8,128)(2,1)} async-done(((bf16[32,128,2048]{2,1,0:T(8,128)(2,1)}), bf16[32,128,2048]{2,1,0:T(8,128)(2,1)}, u32[]{:S(2)}, u32[]{:S(2)}) %all-to-all-start.2) | async-done | bytes 16777248 | tf_op jit(solution)/shard_map/all_to_all | solution.py:231
  1185.3 21.7 %fusion.63 = f32[1024,2048]{1,0:T(8,128)} fusion(bf16[1024,4096]{1,0:T(8,128)(2,1)S(1)} %bitcast.194, bf16[4096,2048]{1,0:T(8,128)(2,1)} %bitcast.13), kind=kOutput, calls=%fused_computation.109 | convolution fusion | flops 17179869184 | bytes 33554432 | tf_op jit(solution)/shard_map/dot_general | solution.py:240
  1207.0 21.8 %fusion.64 = f32[1024,2048]{1,0:T(8,128)} fusion(bf16[1024,4096]{1,0:T(8,128)(2,1)S(1)} %bitcast.192, bf16[4096,2048]{1,0:T(8,128)(2,1)} %bitcast.13), kind=kOutput, calls=%fused_computation.110 | convolution fusion | flops 17179869184 | bytes 33554432 | tf_op jit(solution)/shard_map/dot_general | solution.py:240
  1228.8 28.8 %add_add_fusion.1 = f32[1024,2048]{1,0:T(8,128)} fusion(f32[1024,2048]{1,0:T(8,128)} %fusion.64, f32[1024,2048]{1,0:T(8,128)} %fusion.8, f32[1024,2048]{1,0:T(8,128)} %fusion.63, bf16[1024,4096]{1,0:T(8,128)(2,1)} %get-tuple-element.36, bf16[4096,2048]{1,0:T(8,128)(2,1)} %bitcast.13), kind=kOutput, calls=%fused_computation.46 | convolution fusion | flops 17186160640 | bytes 58720256 | tf_op jit(solution)/shard_map/dot_general | solution.py:240
  1257.7 99.2 %all-to-all-done.3 = bf16[32,128,2048]{2,1,0:T(8,128)(2,1)} async-done(((bf16[32,128,2048]{2,1,0:T(8,128)(2,1)}), bf16[32,128,2048]{2,1,0:T(8,128)(2,1)}, u32[]{:S(2)}, u32[]{:S(2)}) %all-to-all-start.3) | async-done | bytes 16777248 | tf_op jit(solution)/shard_map/all_to_all | solution.py:231
  1356.8 24.0 %fusion.65 = f32[1024,2048]{1,0:T(8,128)} fusion(bf16[1024,4096]{1,0:T(8,128)(2,1)} %get-tuple-element.37, bf16[4096,2048]{1,0:T(8,128)(2,1)} %bitcast.20), kind=kOutput, calls=%fused_computation.111 | convolution fusion | flops 17179869184 | bytes 33554432 | tf_op jit(solution)/shard_map/dot_general | solution.py:240
  1380.9 24.3 %fusion.66 = f32[1024,2048]{1,0:T(8,128)} fusion(bf16[1024,4096]{1,0:T(8,128)(2,1)} %get-tuple-element.40, bf16[4096,2048]{1,0:T(8,128)(2,1)} %bitcast.20), kind=kOutput, calls=%fused_computation.112 | convolution fusion | flops 17179869184 | bytes 33554432 | tf_op jit(solution)/shard_map/dot_general | solution.py:240
  1405.2 28.9 %add_add_fusion = f32[1024,2048]{1,0:T(8,128)} fusion(f32[1024,2048]{1,0:T(8,128)} %fusion.66, f32[1024,2048]{1,0:T(8,128)} %add_add_fusion.1, f32[1024,2048]{1,0:T(8,128)} %fusion.65, bf16[1024,4096]{1,0:T(8,128)(2,1)} %get-tuple-element.41, bf16[4096,2048]{1,0:T(8,128)(2,1)} %bitcast.20), kind=kOutput, calls=%fused_computation.45 | convolution fusion | flops 17186160640 | bytes 58720256 | tf_op jit(solution)/shard_map/dot_general | solution.py:240
  1434.1 19.5 %add_convert_fusion = bf16[1024,2048]{1,0:T(8,128)(2,1)} fusion(f32[1024,2048]{1,0:T(8,128)} %fusion.68, f32[1024,2048]{1,0:T(8,128)} %add_add_fusion, f32[1024,2048]{1,0:T(8,128)} %fusion.67, bf16[1024,2048]{0,1:T(8,128)(2,1)S(1)} %copy-done.2, bf16[2048,2048]{1,0:T(8,128)(2,1)} %bitcast.25), kind=kOutput, calls=%fused_computation.44 | convolution fusion | flops 8598323200 | bytes 41943040 | tf_op jit(solution)/shard_map/dot_general | solution.py:240
  (87 shorter events, 228.1 us)
Async XLA Ops:
  0.0 827.9 %copy-start = (bf16[2048,64]{0,1:T(8,128)(2,1)S(1)}, bf16[2048,64]{0,1:T(8,128)(2,1)}, u32[]{:S(2)}) copy-start(bf16[2048,64]{0,1:T(8,128)(2,1)} %param.9) | copy-start | bytes 786436
  1.0 0.6 copy-start.6
  2.2 375.2 %copy-start.4 = (s32[1024,64]{0,1:T(8,128)}, s32[1024,64]{0,1:T(8,128)S(1)}, u32[]{:S(2)}) copy-start(s32[1024,64]{0,1:T(8,128)S(1)} %fusion.51) | copy-start | bytes 786436
  8.9 368.5 %all-to-all-start = ((s32[32,2,192]{2,1,0:T(2,128)}), s32[32,2,192]{2,1,0:T(2,128)S(1)}, u32[]{:S(2)}, u32[]{:S(2)}) async-start(s32[32,2,192]{2,1,0:T(2,128)} %sub.46), calls=%async_computation | async-start | bytes 131072 | tf_op jit(solution)/shard_map/all_to_all | solution.py:211
  578.7 32.3 %copy-start.8 = (bf16[2,2048,1408]{2,1,0:T(8,128)(2,1)S(1)}, bf16[2,2048,1408]{2,1,0:T(8,128)(2,1)}, u32[]{:S(2)}) copy-start(bf16[2,2048,1408]{2,1,0:T(8,128)(2,1)} %param.11) | copy-start | bytes 34603012
  711.8 104.9 %all-to-all-start.1 = ((bf16[32,64,2048]{2,1,0:T(8,128)(2,1)}), bf16[32,64,2048]{2,1,0:T(8,128)(2,1)}, u32[]{:S(2)}, u32[]{:S(2)}) async-start(bf16[32,64,2048]{2,1,0:T(8,128)(2,1)} %bitcast.190), calls=%async_computation.1 | async-start | bytes 16777216 | tf_op jit(solution)/shard_map/all_to_all | solution.py:231
  816.7 109.7 %all-to-all-start.4 = ((bf16[32,64,2048]{2,1,0:T(8,128)(2,1)}), bf16[32,64,2048]{2,1,0:T(8,128)(2,1)}, u32[]{:S(2)}, u32[]{:S(2)}) async-start(bf16[32,64,2048]{2,1,0:T(8,128)(2,1)} %bitcast.189), calls=%async_computation.4 | async-start | bytes 16777216 | tf_op jit(solution)/shard_map/all_to_all | solution.py:231
  926.3 12.5 copy-start.7
  926.4 12.9 copy-start.5
  926.4 212.5 %all-to-all-start.2 = ((bf16[32,128,2048]{2,1,0:T(8,128)(2,1)}), bf16[32,128,2048]{2,1,0:T(8,128)(2,1)}, u32[]{:S(2)}, u32[]{:S(2)}) async-start(bf16[32,128,2048]{2,1,0:T(8,128)(2,1)} %bitcast.188), calls=%async_computation.2 | async-start | bytes 33554432 | tf_op jit(solution)/shard_map/all_to_all | solution.py:231
  1050.1 13.7 copy-start.1
  1138.8 218.0 %all-to-all-start.3 = ((bf16[32,128,2048]{2,1,0:T(8,128)(2,1)}), bf16[32,128,2048]{2,1,0:T(8,128)(2,1)}, u32[]{:S(2)}, u32[]{:S(2)}) async-start(bf16[32,128,2048]{2,1,0:T(8,128)(2,1)} %bitcast.187), calls=%async_computation.3 | async-start | bytes 33554432 | tf_op jit(solution)/shard_map/all_to_all | solution.py:231
  1156.9 14.8 %copy-start.3 = (bf16[1024,2048]{0,1:T(8,128)(2,1)S(1)}, bf16[1024,2048]{0,1:T(8,128)(2,1)}, u32[]{:S(2)}) copy-start(bf16[1024,2048]{0,1:T(8,128)(2,1)} %get-tuple-element.45) | copy-start | bytes 12582916
  1156.9 28.4 %slice-start.2 = ((s8[8388608]{0:T(1024)(128)(4,1)}), s8[4194304]{0:T(1024)(128)(4,1)S(1)}, s32[]{:S(2)}) async-start(s8[8388608]{0:T(1024)(128)(4,1)} %bitcast.193), calls=%async_computation.7 | async-start | bytes 8388608
  1171.6 13.7 slice-start.3
  1171.6 35.4 %slice-start = ((s8[8388608]{0:T(1024)(128)(4,1)}), s8[4194304]{0:T(1024)(128)(4,1)S(1)}, s32[]{:S(2)}) async-start(s8[8388608]{0:T(1024)(128)(4,1)} %bitcast.191), calls=%async_computation.5 | async-start | bytes 8388608
  1185.3 21.7 %slice-start.1 = ((s8[8388608]{0:T(1024)(128)(4,1)}), s8[4194304]{0:T(1024)(128)(4,1)S(1)}, s32[]{:S(2)}) async-start(s8[8388608]{0:T(1024)(128)(4,1)} %bitcast.191), calls=%async_computation.6 | async-start | bytes 8388608
  1405.2 28.9 %copy-start.2 = (bf16[1024,2048]{0,1:T(8,128)(2,1)S(1)}, bf16[1024,2048]{0,1:T(8,128)(2,1)}, u32[]{:S(2)}) copy-start(bf16[1024,2048]{0,1:T(8,128)(2,1)} %get-tuple-element.46) | copy-start | bytes 12582916
